TPU v7x, 32 devices: a whole 2x2x4 slice. The times are simulated.
32 devices in a mesh: row: 4 (over z), col: 8 (over y, x, core).
Axes of the slice: x: 2, y: 2, z: 4, core: 2. Of those that a mesh axis runs over, the one named last changes fastest.
Arguments:
- front: float32 [12288, 12288], P('row', 'col'), as said below
- structure: int32 [3, 96], replicated, may hold values from 0 to 1, as said below
- factor_front: float32 [3, 12288, 512], P(None, 'row', 'col'), may hold values from -0.0546875 to 0.0546875
- factor_border: float32 [2, 512, 512], replicated, may hold values from -0.6 to 0.6
- pivot_inverse: float32 [3, 512, 512], P(None, 'row')
Outputs:
- inverse_front: float32 [3, 512, 12288], P(None, 'row', 'col')
- inverse_parent: float32 [2, 512, 512], P(None, 'row')
- inverse_diagonal: float32 [3, 512, 512], P(None, 'row')
Inputs may be any that keep to these rules, and one draw needn't show every extreme that they name: front is exactly symmetric. structure[k, b] = 1 where front block b (rows b * 128 to (b + 1) * 128 - 1) lies in supernode k's structure; every 1 in row k is also a 1 in row k - 1; blocks b < 24 are 1 in every row.
All inputs are finite; a program needn't handle non-finite values.
Results may differ from a plain program's by a relative error of at most 0.0001.
Values sent between devices are 32-bit elements; how exact they have to be, the bound alone decides.
No kernel may reach another device: no remote copies, remote signals or barrier semaphores. Data moves between devices by JAX's collectives and lax.ppermute only.
A program may use at most 128 MiB of HBM per device.

v0:
```python
import jax
import jax.numpy as jnp
from jax import lax
from jax.sharding import PartitionSpec as P

BLK = 128
HIGH = lax.Precision.HIGHEST


def broadcast(x, axis, root):
    mine = lax.axis_index(axis) == root
    return lax.psum(jnp.where(mine, x, jnp.zeros_like(x)), axis)


def matmul(former, latter):
    return jnp.dot(former, latter, precision=HIGH, preferred_element_type=jnp.float32)


def contract_first(former, latter):
    return lax.dot_general(
        former, latter, (((0,), (0,)), ((), ())), precision=HIGH, preferred_element_type=jnp.float32
    )


def block_flags(structure_row, first_row, rows_count):
    position = first_row + jnp.arange(rows_count, dtype=jnp.int32)
    owners = position // BLK
    numbers = jnp.arange(structure_row.shape[0], dtype=jnp.int32)
    matches = (owners[:, None] == numbers[None, :]).astype(jnp.float32)
    return jnp.dot(matches, structure_row.astype(jnp.float32), precision=HIGH)


def body(front, structure, factor_front, factor_border, pivot_inverse):
    row_index = lax.axis_index("row")
    col_index = lax.axis_index("col")
    rows_here = front.shape[0]
    cols_here = front.shape[1]
    width_here = pivot_inverse.shape[1]
    supers = structure.shape[0]
    row_first = row_index * rows_here
    col_first = col_index * cols_here
    fronts = []
    parents = []
    diagonals = []
    previous = None
    diag_prev = None
    for section in range(supers):
        gathered = lax.all_gather(factor_front[section], "col", axis=1, tiled=True)
        row_flags = block_flags(structure[section], row_first, rows_here)
        factor_rows = gathered * row_flags[:, None]
        own_half = lax.dynamic_slice_in_dim(factor_rows, col_index % 2 * cols_here, cols_here, 0)
        factor_cols = broadcast(own_half, "row", col_index // 2)
        partial_value = contract_first(factor_rows, front)
        if section > 0:
            border = factor_border[section - 1]
            border_rows = lax.dynamic_slice_in_dim(border, row_index * width_here, width_here, 0)
            partial_value = partial_value + contract_first(border_rows, previous)
            parent_part = lax.psum(matmul(previous, factor_cols), "col")
            parent_rows = parent_part + matmul(diag_prev, border)
            parent_all = lax.all_gather(parent_rows, "row", axis=0, tiled=True)
            parents.append(-parent_rows)
        image_rows = lax.psum_scatter(partial_value, "row", scatter_dimension=0, tiled=True)
        col_flags = block_flags(structure[section], col_first, cols_here)
        current = -(image_rows * col_flags[None, :])
        gram_rows = lax.psum(matmul(image_rows, factor_cols), "col")
        diag_now = pivot_inverse[section] + gram_rows
        if section > 0:
            parent_slice = lax.dynamic_slice_in_dim(
                parent_all, row_index * width_here, width_here, 1
            )
            diag_now = diag_now + contract_first(parent_slice, border)
        fronts.append(current)
        diagonals.append(diag_now)
        previous = current
        diag_prev = diag_now
    return (jnp.stack(fronts), jnp.stack(parents), jnp.stack(diagonals))


def solution(mesh):
    placed = (P("row", "col"), P(), P(None, "row", "col"), P(), P(None, "row", None))
    return jax.shard_map(
        body,
        mesh=mesh,
        in_specs=placed,
        out_specs=(P(None, "row", "col"), P(None, "row", None), P(None, "row", None)),
        check_vma=False,
    )
```

profile of v0, /device:TPU:0, one launch (start us, length us, event | category | flops | bytes accessed | tf_op | source)
XLA Modules:
  0.0 802.7 jit_solution(8092300581253794925)
XLA Ops:
  7.2 3.1 fusion.61
  13.2 45.4 %all-gather.13.cloned.1.call-done = f32[1,3072,512]{1,2,0:T(8,128)} async-done(((f32[1,3072,64]{1,2,0:T(8,128)}), f32[1,3072,512]{1,2,0:T(8,128)}) %all-gather.13.cloned.1.call-update) | async-done | bytes 6291472 | tf_op jit(solution)/shard_map/all_gather | solution.py:48
  58.6 3.4 bitcast_multiply_fusion.2
  62.0 2.6 copy-done.1
  64.7 33.4 %fusion.63 = f32[512,1536]{1,0:T(8,128)} fusion(f32[3072,512]{0,1:T(8,128)S(1)} %bitcast_multiply_fusion.2, f32[3072,1536]{1,0:T(8,128)} %param.5), kind=kOutput, calls=%fused_computation.103 | convolution fusion | flops 28991029248 | bytes 28311552 | tf_op jit(solution)/shard_map/dot_general | solution.py:20
  103.0 2.9 all-gather.15.cloned.1.call-done
  105.9 3.4 bitcast_multiply_fusion.1
  109.3 2.6 copy-done.2
  111.9 33.4 %fusion.64 = f32[512,1536]{1,0:T(8,128)} fusion(f32[3072,512]{0,1:T(8,128)S(1)} %bitcast_multiply_fusion.1, f32[3072,1536]{1,0:T(8,128)} %param.5), kind=kOutput, calls=%fused_computation.104 | convolution fusion | flops 28991029248 | bytes 28311552 | tf_op jit(solution)/shard_map/dot_general | solution.py:20
  145.3 23.4 %reduce-scatter.4.cloned.1.call-done = f32[128,1536]{1,0:T(8,128)} async-done(((f32[512,1536]{1,0:T(8,128)}), f32[128,1536]{1,0:T(8,128)}) %reduce-scatter.4.cloned.1.call-update) | async-done | bytes 786448 | tf_op jit(solution)/shard_map/reduce_scatter | solution.py:62
  168.6 6.6 convolution_add_fusion.1
  177.5 4.1 dynamic-slice_select_fusion.2
  181.6 3.8 dynamic-slice_select_fusion.1
  185.4 30.3 %all-gather.17.cloned.1.call-done = f32[1,3072,512]{1,2,0:T(8,128)} async-done(((f32[1,3072,64]{1,2,0:T(8,128)}), f32[1,3072,512]{1,2,0:T(8,128)}) %all-gather.17.cloned.1.call-update) | async-done | bytes 6291472 | tf_op jit(solution)/shard_map/all_gather | solution.py:48
  215.7 3.4 bitcast_multiply_fusion
  219.1 2.6 copy-done.3
  224.4 35.4 %fusion.65 = f32[512,1536]{1,0:T(8,128)} fusion(f32[3072,512]{0,1:T(8,128)} %copy-done.3, f32[3072,1536]{1,0:T(8,128)} %param.5), kind=kOutput, calls=%fused_computation.105 | convolution fusion | flops 28991029248 | bytes 28311552 | tf_op jit(solution)/shard_map/dot_general | solution.py:20
  259.8 18.5 %reduce-scatter.6.cloned.1.call-done = f32[128,1536]{1,0:T(8,128)} async-done(((f32[512,1536]{1,0:T(8,128)}), f32[128,1536]{1,0:T(8,128)}) %reduce-scatter.6.cloned.1.call-update) | async-done | bytes 786448 | tf_op jit(solution)/shard_map/reduce_scatter | solution.py:62
  278.3 5.6 convolution_add_fusion
  284.2 321.4 %all-reduce.7.cloned.1.call-done = (f32[1536,512]{0,1:T(8,128)}, f32[1536,512]{0,1:T(8,128)}, f32[1536,512]{0,1:T(8,128)}) async-done(((f32[1536,512]{0,1:T(8,128)}, f32[1536,512]{0,1:T(8,128)}, f32[1536,512]{0,1:T(8,128)}), (f32[1536,512]{0,1:T(8,128)}, f32[1536,512]{0,1:T(8,128)}, f32[1536,512]{0,1:T(8,128)})) %all-reduce.7.cloned.1.call-update) | async-done | bytes 9437200 | tf_op jit(solution)/shard_map/psum | solution.py:12
  605.6 6.0 fusion.66
  611.6 3.9 fusion.11
  615.5 4.0 fusion.67
  619.6 3.9 fusion.13
  623.4 43.9 %reduce-scatter.8.cloned.1.call-done = f32[128,1536]{1,0:T(8,128)} async-done(((f32[512,1536]{1,0:T(8,128)}), f32[128,1536]{1,0:T(8,128)}) %reduce-scatter.8.cloned.1.call-update) | async-done | bytes 786448 | tf_op jit(solution)/shard_map/reduce_scatter | solution.py:62
  667.3 6.1 fusion.68
  673.8 58.5 %all-reduce.5.cloned.1.call-done = (f32[128,512]{1,0:T(8,128)}, f32[128,512]{1,0:T(8,128)}, f32[128,512]{1,0:T(8,128)}, f32[128,512]{1,0:T(8,128)}, f32[128,512]{1,0:T(8,128)}) async-done(((f32[128,512]{1,0:T(8,128)}, f32[128,512]{1,0:T(8,128)}, f32[128,512]{1,0:T(8,128)}, f32[128,512]{1,0:T(8,128)}, f32[128,512]{1,0:T(8,128)}), (f32[128,512]{1,0:T(8,128)}, f32[128,512]{1,0:T(8,128)}, f32[128,512]{1,0:T(8,128)}, ...) | async-done | bytes 1310736 | tf_op jit(solution)/shard_map/psum | solution.py:58
  732.3 2.5 convolution_add_fusion.5
  736.5 2.2 fusion.14
  738.7 23.4 %all-gather.9.cloned.1.call-done = f32[512,512]{1,0:T(8,128)} async-done(((f32[128,512]{1,0:T(8,128)}), f32[512,512]{1,0:T(8,128)}) %all-gather.9.cloned.1.call-update) | async-done | bytes 1048592 | tf_op jit(solution)/shard_map/all_gather | solution.py:60
  765.5 3.0 pad_maximum_fusion
  770.4 22.5 %all-gather.11.cloned.1.call-done = f32[512,512]{1,0:T(8,128)} async-done(((f32[128,512]{1,0:T(8,128)}), f32[512,512]{1,0:T(8,128)}) %all-gather.11.cloned.1.call-update) | async-done | bytes 1048592 | tf_op jit(solution)/shard_map/all_gather | solution.py:60
  (67 shorter events, 22.8 us)
Async XLA Ops:
  7.2 4.0 copy-start.14
  7.2 51.4 %all-gather.13.cloned.1.call-start = ((), (), s32[]{:S(2)}) async-start(), calls=%async_computation.8 | async-start | bytes 7077888 | tf_op jit(solution)/shard_map/all_gather | solution.py:48
  10.3 95.6 %all-gather.15.cloned.1.call-start = ((), (), s32[]{:S(2)}) async-start(), calls=%async_computation.9 | async-start | bytes 7077888 | tf_op jit(solution)/shard_map/all_gather | solution.py:48
  11.1 157.6 %reduce-scatter.4.cloned.1.call-start = ((), (), s32[]{:S(2)}) async-start(), calls=%async_computation.3 | async-start | bytes 3932160 | tf_op jit(solution)/shard_map/reduce_scatter | solution.py:62
  62.0 2.7 copy-start.1
  98.0 3.8 copy-start
  98.1 117.6 %all-gather.17.cloned.1.call-start = ((), (), s32[]{:S(2)}) async-start(), calls=%async_computation.10 | async-start | bytes 7077888 | tf_op jit(solution)/shard_map/all_gather | solution.py:48
  98.6 179.6 %reduce-scatter.6.cloned.1.call-start = ((), (), s32[]{:S(2)}) async-start(), calls=%async_computation.4 | async-start | bytes 3932160 | tf_op jit(solution)/shard_map/reduce_scatter | solution.py:62
  109.3 2.6 copy-start.2
  175.3 430.3 %all-reduce.7.cloned.1.call-start = ((), (), s32[]{:S(2)}) async-start(), calls=%async_computation.12 | async-start | bytes 18874368 | tf_op jit(solution)/shard_map/psum | solution.py:12
  219.1 2.7 copy-start.3
  223.7 443.5 %reduce-scatter.8.cloned.1.call-start = ((), (), s32[]{:S(2)}) async-start(), calls=%async_computation.5 | async-start | bytes 3932160 | tf_op jit(solution)/shard_map/reduce_scatter | solution.py:62
  283.9 321.7 %copy-start.4 = (f32[128,1536]{1,0:T(8,128)S(1)}, f32[128,1536]{1,0:T(8,128)}, u32[]{:S(2)}) copy-start(f32[128,1536]{1,0:T(8,128)} %reduce-scatter.4.cloned.1.call-done) | copy-start | bytes 2359300
  284.0 448.3 %all-reduce.5.cloned.1.call-start = ((), (), s32[]{:S(2)}) async-start(), calls=%async_computation.11 | async-start | bytes 2621440 | tf_op jit(solution)/shard_map/psum | solution.py:58
  605.6 6.0 copy-start.7
  611.6 3.9 copy-start.5
  615.5 4.0 copy-start.6
  673.5 88.6 %all-gather.9.cloned.1.call-start = ((), (), s32[]{:S(2)}) async-start(), calls=%async_computation.6 | async-start | bytes 1310720 | tf_op jit(solution)/shard_map/all_gather | solution.py:60
  734.8 29.1 %copy-start.13 = (f32[128,512]{1,0:T(8,128)S(1)}, f32[128,512]{1,0:T(8,128)}, u32[]{:S(2)}) copy-start(f32[128,512]{1,0:T(8,128)} %get-tuple-element.3) | copy-start | bytes 786436
  734.8 58.1 %all-gather.11.cloned.1.call-start = ((), (), s32[]{:S(2)}) async-start(), calls=%async_computation.7 | async-start | bytes 1310720 | tf_op jit(solution)/shard_map/all_gather | solution.py:60
  736.5 28.9 %copy-start.8 = (f32[128,1536]{1,0:T(8,128)S(1)}, f32[128,1536]{1,0:T(8,128)}, u32[]{:S(2)}) copy-start(f32[128,1536]{1,0:T(8,128)} %reduce-scatter.8.cloned.1.call-done) | copy-start | bytes 2359300
  765.4 3.1 copy-start.10
  765.4 3.1 copy-start.11
  765.5 4.0 copy-start.9
  765.5 27.4 %copy-start.12 = (f32[128,512]{1,0:T(8,128)S(1)}, f32[128,512]{1,0:T(8,128)}, u32[]{:S(2)}) copy-start(f32[128,512]{1,0:T(8,128)} %get-tuple-element.7) | copy-start | bytes 786436
Sparse Core Ops, SparseCore 0:
  10.5 48.1 all-gather.12
  60.5 45.3 all-gather.14
  108.2 60.3 reduce-scatter.3
  170.4 45.2 all-gather.16
  217.9 60.3 reduce-scatter.5
  281.0 324.5 all-reduce.6
  607.9 59.3 reduce-scatter.7
  673.6 58.6 all-reduce.4
  735.0 27.0 all-gather.8
  765.5 27.3 all-gather.10
where the time goes:
time: 809 us; the launch traced here: 803 us
  waiting for transfers between devices  591 us (73%)
  matrix products  154 us (19%)
  other arithmetic  29 us (4%)
  between operations  14.7 us (2%)
  local copies, waits for them, and re-layouts  12.1 us (1%)
    psum x1, waiting for transfers between devices, broadcast(): return lax.psum(jnp.where(mine, x, jnp.zeros_like(x)), axis)  321 us
    dot_general x7, matrix products, contract_first(): lax.dot_general(former, latter, (((0,), (0,)), ((), ())), precision=HIGH,...  118 us
    reduce_scatter x3, waiting for transfers between devices, body(): lax.psum_scatter(partial_value, 'row', scatter_dimension=0, tiled=True)  85.7 us
    all_gather x3, waiting for transfers between devices, body(): gathered = lax.all_gather(factor_front[section], 'col', axis=1, tiled=True)  78.7 us
    psum x1, waiting for transfers between devices, body(): parent_part = lax.psum(matmul(previous, factor_cols), 'col')  58.5 us
    all_gather x2, waiting for transfers between devices, body(): parent_all = lax.all_gather(parent_rows, 'row', axis=0, tiled=True)  45.9 us
    dot_general x7, matrix products, matmul(): jnp.dot(former, latter, precision=HIGH, preferred_element_type=jnp.float32)  27.9 us
  transfers between devices with their start and end apart: 10, of which 10 were waited for; matrix products, arithmetic and copies ran while one was open for 21% of the time, Pallas kernels for 0%

commit v1 on v0

--- a/solution.py
+++ b/solution.py
@@ -9,7 +9,7 @@
 
 def broadcast(x, axis, root):
     mine = lax.axis_index(axis) == root
-    return lax.psum(jnp.where(mine, x, jnp.zeros_like(x)), axis)
+    return jnp.sum(lax.all_gather(jnp.where(mine, x, jnp.zeros_like(x)), axis), 0)
 
 
 def matmul(former, latter):

time: 809 us -> 1140 us (1.41)
  waiting for transfers between devices: 591 us -> 841 us
  local copies, waits for them, and re-layouts: 12.1 us -> 60.2 us
  other arithmetic: 29 us -> 65.4 us
    all_gather x0 -> x3, waiting for transfers between devices: none -> 594 us  [broadcast(): lax.all_gather(jnp.where(mine, x, jnp.zeros_like(x)), axis)]
    psum x1 -> x0, waiting for transfers between devices: 321 us -> none  [broadcast(): return lax.psum(jnp.where(mine, x, jnp.zeros_like(x)), axis)]
    all_gather x0 -> x3, local copies, waits for them, and re-layouts: none -> 47.7 us  [broadcast(): lax.all_gather(jnp.where(mine, x, jnp.zeros_like(x)), axis)]
    reduce_sum x0 -> x3, other arithmetic: none -> 36.5 us  [broadcast(): jnp.sum(lax.all_gather(jnp.where(mine, x, jnp.zeros_like(x)), axis), 0)]
    reduce_scatter x3, waiting for transfers between devices: 85.7 us -> 53.3 us  [body(): lax.psum_scatter(partial_value, 'row', scatter_dimension=0, tiled=True)]
  transfers between devices with their start and end apart: 10 -> 12, of which waited for: 10 -> 12; matrix products, arithmetic and copies ran while one was open for 21% -> 22% of each run, Pallas kernels for 0% -> 0%
where the time goes in v1:
time: 1140 us; the launch traced here: 1130 us
  waiting for transfers between devices  841 us (74%)
  matrix products  151 us (13%)
  other arithmetic  65.4 us (6%)
  local copies, waits for them, and re-layouts  60.2 us (5%)
  between operations  14.8 us (1%)
    all_gather x3, waiting for transfers between devices, broadcast(): lax.all_gather(jnp.where(mine, x, jnp.zeros_like(x)), axis)  594 us
    dot_general x7, matrix products, contract_first(): lax.dot_general(former, latter, (((0,), (0,)), ((), ())), precision=HIGH,...  116 us
    all_gather x3, waiting for transfers between devices, body(): gathered = lax.all_gather(factor_front[section], 'col', axis=1, tiled=True)  87.6 us
    psum x1, waiting for transfers between devices, body(): parent_part = lax.psum(matmul(previous, factor_cols), 'col')  58.6 us
    reduce_scatter x3, waiting for transfers between devices, body(): lax.psum_scatter(partial_value, 'row', scatter_dimension=0, tiled=True)  53.3 us
    all_gather x3, local copies, waits for them, and re-layouts, broadcast(): lax.all_gather(jnp.where(mine, x, jnp.zeros_like(x)), axis)  47.7 us
    all_gather x2, waiting for transfers between devices, body(): parent_all = lax.all_gather(parent_rows, 'row', axis=0, tiled=True)  45.9 us
    reduce_sum x3, other arithmetic, broadcast(): jnp.sum(lax.all_gather(jnp.where(mine, x, jnp.zeros_like(x)), axis), 0)  36.5 us
  transfers between devices with their start and end apart: 12, of which 12 were waited for; matrix products, arithmetic and copies ran while one was open for 22% of the time, Pallas kernels for 0%

profile of v1, /device:TPU:0, one launch (start us, length us, event | category | flops | bytes accessed | tf_op | source)
XLA Modules:
  0.0 1133.4 jit_solution(8649520426344873336)
XLA Ops:
  13.2 45.4 %all-gather.19.cloned.1.call-done = f32[1,3072,512]{1,2,0:T(8,128)} async-done(((f32[1,3072,64]{1,2,0:T(8,128)}), f32[1,3072,512]{1,2,0:T(8,128)}) %all-gather.19.cloned.1.call-update) | async-done | bytes 6291472 | tf_op jit(solution)/shard_map/all_gather | solution.py:48
  58.6 3.4 bitcast_multiply_fusion.2
  64.7 33.4 %fusion.63 = f32[512,1536]{1,0:T(8,128)} fusion(f32[3072,512]{0,1:T(8,128)S(1)} %bitcast_multiply_fusion.2, f32[3072,1536]{1,0:T(8,128)} %param.5), kind=kOutput, calls=%fused_computation.103 | convolution fusion | flops 28991029248 | bytes 28311552 | tf_op jit(solution)/shard_map/dot_general | solution.py:20
  105.9 3.4 bitcast_multiply_fusion.1
  111.9 34.1 %fusion.64 = f32[512,1536]{1,0:T(8,128)S(1)} fusion(f32[3072,512]{0,1:T(8,128)S(1)} %bitcast_multiply_fusion.1, f32[3072,1536]{1,0:T(8,128)} %param.5), kind=kOutput, calls=%fused_computation.104 | convolution fusion | flops 28991029248 | bytes 28311552 | tf_op jit(solution)/shard_map/dot_general | solution.py:20
  146.0 22.7 %reduce-scatter.4.cloned.1.call-done = f32[128,1536]{1,0:T(8,128)} async-done(((f32[512,1536]{1,0:T(8,128)}), f32[128,1536]{1,0:T(8,128)}) %reduce-scatter.4.cloned.1.call-update) | async-done | bytes 786448 | tf_op jit(solution)/shard_map/reduce_scatter | solution.py:62
  168.7 5.6 convolution_add_fusion.1
  176.4 39.3 %all-gather.23.cloned.1.call-done = f32[1,3072,512]{1,2,0:T(8,128)} async-done(((f32[1,3072,64]{1,2,0:T(8,128)}), f32[1,3072,512]{1,2,0:T(8,128)}) %all-gather.23.cloned.1.call-update) | async-done | bytes 6291472 | tf_op jit(solution)/shard_map/all_gather | solution.py:48
  215.7 3.4 bitcast_multiply_fusion
  223.7 4.0 dynamic-slice_select_fusion.2
  227.8 3.8 dynamic-slice_select_fusion.1
  232.3 33.8 %fusion.65 = f32[512,1536]{1,0:T(8,128)S(1)} fusion(f32[3072,512]{0,1:T(8,128)} %copy-done.5, f32[3072,1536]{1,0:T(8,128)} %param.5), kind=kOutput, calls=%fused_computation.105 | convolution fusion | flops 28991029248 | bytes 28311552 | tf_op jit(solution)/shard_map/dot_general | solution.py:20
  266.1 12.2 %reduce-scatter.6.cloned.1.call-done = f32[128,1536]{1,0:T(8,128)} async-done(((f32[512,1536]{1,0:T(8,128)}), f32[128,1536]{1,0:T(8,128)}) %reduce-scatter.6.cloned.1.call-update) | async-done | bytes 786448 | tf_op jit(solution)/shard_map/reduce_scatter | solution.py:62
  278.3 5.5 convolution_add_fusion
  283.9 214.0 %all-gather.29.cloned.1.call-done = f32[6144,512]{0,1:T(8,128)} async-done(((f32[1536,512]{0,1:T(8,128)}), f32[6144,512]{0,1:T(8,128)}) %all-gather.29.cloned.1.call-update) | async-done | bytes 12582928 | tf_op jit(solution)/shard_map/all_gather | solution.py:12
  497.9 16.3 %reshape.60 = f32[4,1536,512]{1,0,2:T(4,128)} reshape(f32[6144,512]{0,1:T(8,128)} %all-gather.29.cloned.1.call-done) | data formatting | bytes 25165824 | tf_op jit(solution)/shard_map/all_gather | solution.py:12
  514.1 11.0 reduce_sum.29
  525.1 190.7 %all-gather.25.cloned.1.call-done = f32[6144,512]{0,1:T(8,128)} async-done(((f32[1536,512]{0,1:T(8,128)}), f32[6144,512]{0,1:T(8,128)}) %all-gather.25.cloned.1.call-update) | async-done | bytes 12582928 | tf_op jit(solution)/shard_map/all_gather | solution.py:12
  715.8 15.8 %reshape.58 = f32[4,1536,512]{1,0,2:T(4,128)} reshape(f32[6144,512]{0,1:T(8,128)} %all-gather.25.cloned.1.call-done) | data formatting | bytes 25165824 | tf_op jit(solution)/shard_map/all_gather | solution.py:12
  731.6 12.7 %reduce_sum.27 = f32[1536,512]{0,1:T(8,128)} reduce(f32[4,1536,512]{1,0,2:T(4,128)} %reshape.58, f32[]{:T(128)} %constant.82.clone.1), dimensions={0}, to_apply=%region_3.4 | reduce | flops 2359296 | bytes 15728644 | tf_op jit(solution)/shard_map/reduce_sum | solution.py:12
  744.3 189.5 %all-gather.27.cloned.1.call-done = f32[6144,512]{0,1:T(8,128)} async-done(((f32[1536,512]{0,1:T(8,128)}), f32[6144,512]{0,1:T(8,128)}) %all-gather.27.cloned.1.call-update) | async-done | bytes 12582928 | tf_op jit(solution)/shard_map/all_gather | solution.py:12
  933.8 15.6 %reshape.59 = f32[4,1536,512]{1,0,2:T(4,128)} reshape(f32[6144,512]{0,1:T(8,128)} %all-gather.27.cloned.1.call-done) | data formatting | bytes 25165824 | tf_op jit(solution)/shard_map/all_gather | solution.py:12
  949.4 12.8 %reduce_sum.28 = f32[1536,512]{0,1:T(8,128)} reduce(f32[4,1536,512]{1,0,2:T(4,128)} %reshape.59, f32[]{:T(128)} %constant.82.clone.1), dimensions={0}, to_apply=%region_5.6 | reduce | flops 2359296 | bytes 15728644 | tf_op jit(solution)/shard_map/reduce_sum | solution.py:12
  962.3 6.3 fusion.67
  968.5 3.9 fusion.11
  972.4 3.9 fusion.13
  976.3 18.4 %reduce-scatter.8.cloned.1.call-done = f32[128,1536]{1,0:T(8,128)} async-done(((f32[512,1536]{1,0:T(8,128)}), f32[128,1536]{1,0:T(8,128)}) %reduce-scatter.8.cloned.1.call-update) | async-done | bytes 786448 | tf_op jit(solution)/shard_map/reduce_scatter | solution.py:62
  994.7 5.3 fusion.68
  1000.0 4.0 fusion.66
  1004.4 58.6 %all-reduce.3.cloned.1.call-done = (f32[128,512]{1,0:T(8,128)}, f32[128,512]{1,0:T(8,128)}, f32[128,512]{1,0:T(8,128)}, f32[128,512]{1,0:T(8,128)}, f32[128,512]{1,0:T(8,128)}) async-done(((f32[128,512]{1,0:T(8,128)}, f32[128,512]{1,0:T(8,128)}, f32[128,512]{1,0:T(8,128)}, f32[128,512]{1,0:T(8,128)}, f32[128,512]{1,0:T(8,128)}), (f32[128,512]{1,0:T(8,128)}, f32[128,512]{1,0:T(8,128)}, f32[128,512]{1,0:T(8,128)}, ...) | async-done | bytes 1310736 | tf_op jit(solution)/shard_map/psum | solution.py:58
  1069.3 23.4 %all-gather.15.cloned.1.call-done = f32[512,512]{1,0:T(8,128)} async-done(((f32[128,512]{1,0:T(8,128)}), f32[512,512]{1,0:T(8,128)}) %all-gather.15.cloned.1.call-update) | async-done | bytes 1048592 | tf_op jit(solution)/shard_map/all_gather | solution.py:60
  1101.1 22.5 %all-gather.17.cloned.1.call-done = f32[512,512]{1,0:T(8,128)} async-done(((f32[128,512]{1,0:T(8,128)}), f32[512,512]{1,0:T(8,128)}) %all-gather.17.cloned.1.call-update) | async-done | bytes 1048592 | tf_op jit(solution)/shard_map/all_gather | solution.py:60
  (85 shorter events, 44.0 us)
Async XLA Ops:
  7.2 4.0 copy-start.17
  7.2 51.4 %all-gather.19.cloned.1.call-start = ((), (), s32[]{:S(2)}) async-start(), calls=%async_computation.8 | async-start | bytes 7077888 | tf_op jit(solution)/shard_map/all_gather | solution.py:48
  10.4 95.6 %all-gather.21.cloned.1.call-start = ((), (), s32[]{:S(2)}) async-start(), calls=%async_computation.9 | async-start | bytes 7077888 | tf_op jit(solution)/shard_map/all_gather | solution.py:48
  11.1 157.6 %reduce-scatter.4.cloned.1.call-start = ((), (), s32[]{:S(2)}) async-start(), calls=%async_computation.3 | async-start | bytes 3932160 | tf_op jit(solution)/shard_map/reduce_scatter | solution.py:62
  62.0 2.6 copy-start.3
  98.1 3.5 copy-start.1
  98.1 117.6 %all-gather.23.cloned.1.call-start = ((), (), s32[]{:S(2)}) async-start(), calls=%async_computation.10 | async-start | bytes 7077888 | tf_op jit(solution)/shard_map/all_gather | solution.py:48
  98.7 179.6 %reduce-scatter.6.cloned.1.call-start = ((), (), s32[]{:S(2)}) async-start(), calls=%async_computation.4 | async-start | bytes 3932160 | tf_op jit(solution)/shard_map/reduce_scatter | solution.py:62
  109.3 2.6 copy-start.4
  174.3 323.5 %all-gather.29.cloned.1.call-start = ((), (), s32[]{:S(2)}) async-start(), calls=%async_computation.13 | async-start | bytes 15728640 | tf_op jit(solution)/shard_map/all_gather | solution.py:12
  219.1 2.6 copy-start.5
  223.7 492.2 %all-gather.25.cloned.1.call-start = ((), (), s32[]{:S(2)}) async-start(), calls=%async_computation.11 | async-start | bytes 15728640 | tf_op jit(solution)/shard_map/all_gather | solution.py:12
  227.7 706.1 %all-gather.27.cloned.1.call-start = ((), (), s32[]{:S(2)}) async-start(), calls=%async_computation.12 | async-start | bytes 15728640 | tf_op jit(solution)/shard_map/all_gather | solution.py:12
  231.6 763.1 %reduce-scatter.8.cloned.1.call-start = ((), (), s32[]{:S(2)}) async-start(), calls=%async_computation.5 | async-start | bytes 3932160 | tf_op jit(solution)/shard_map/reduce_scatter | solution.py:62
  283.8 779.1 %all-reduce.3.cloned.1.call-start = ((), (), s32[]{:S(2)}) async-start(), calls=%async_computation.14 | async-start | bytes 2621440 | tf_op jit(solution)/shard_map/psum | solution.py:58
  962.3 6.3 copy-start
  962.3 6.3 copy-start.6
  968.5 3.9 copy-start.9
  994.7 5.3 copy-start.7
  994.7 5.3 copy-start.10
  1000.0 62.9 %copy-start.2 = (f32[2,512,512]{2,1,0:T(8,128)S(1)}, f32[2,512,512]{2,1,0:T(8,128)}, u32[]{:S(2)}) copy-start(f32[2,512,512]{2,1,0:T(8,128)} %param.8) | copy-start | bytes 6291460
  1000.0 66.1 %copy-start.8 = (f32[128,1536]{1,0:T(8,128)S(1)}, f32[128,1536]{1,0:T(8,128)}, u32[]{:S(2)}) copy-start(f32[128,1536]{1,0:T(8,128)} %reduce-scatter.4.cloned.1.call-done) | copy-start | bytes 2359300
  1004.1 88.6 %all-gather.15.cloned.1.call-start = ((), (), s32[]{:S(2)}) async-start(), calls=%async_computation.6 | async-start | bytes 1310720 | tf_op jit(solution)/shard_map/all_gather | solution.py:60
  1065.5 29.1 %copy-start.16 = (f32[128,512]{1,0:T(8,128)S(1)}, f32[128,512]{1,0:T(8,128)}, u32[]{:S(2)}) copy-start(f32[128,512]{1,0:T(8,128)} %get-tuple-element.3) | copy-start | bytes 786436
  1065.5 58.1 %all-gather.17.cloned.1.call-start = ((), (), s32[]{:S(2)}) async-start(), calls=%async_computation.7 | async-start | bytes 1310720 | tf_op jit(solution)/shard_map/all_gather | solution.py:60
  1067.2 28.9 %copy-start.11 = (f32[128,1536]{1,0:T(8,128)S(1)}, f32[128,1536]{1,0:T(8,128)}, u32[]{:S(2)}) copy-start(f32[128,1536]{1,0:T(8,128)} %reduce-scatter.8.cloned.1.call-done) | copy-start | bytes 2359300
  1096.1 3.1 copy-start.13
  1096.1 3.1 copy-start.14
  1096.2 4.0 copy-start.12
  1096.2 27.4 %copy-start.15 = (f32[128,512]{1,0:T(8,128)S(1)}, f32[128,512]{1,0:T(8,128)}, u32[]{:S(2)}) copy-start(f32[128,512]{1,0:T(8,128)} %get-tuple-element.7) | copy-start | bytes 786436
Sparse Core Ops, SparseCore 0:
  10.5 48.1 all-gather.18
  60.5 45.3 all-gather.20
  108.2 60.3 reduce-scatter.3
  170.4 45.2 all-gather.22
  217.9 60.3 reduce-scatter.5
  279.7 218.0 all-gather.28
  499.4 216.3 all-gather.24
  717.4 216.3 all-gather.26
  936.1 58.5 reduce-scatter.7
  1004.2 58.6 all-reduce.2
  1065.6 27.0 all-gather.14
  1096.2 27.3 all-gather.16
